TPU v7x, 32 devices: a whole 2x2x4 slice. The times are simulated.
32 devices in a mesh: tm: 8 (over z, y), sym: 4 (over x, core).
Axes of the slice: x: 2, y: 2, z: 4, core: 2. Of those that a mesh axis runs over, the one named last changes fastest.
Arguments:
- trade_age: float32 [65536], P(('tm', 'sym')), may hold values from 0.02 to 20
- trade_size: float32 [65536], P(('tm', 'sym')), may hold values from 0.5 to 4
- owner: int32 [65536, 1], P(('tm', 'sym')), may hold values from 0 to 31; in each aligned block of 2048 rows (0 to 2047, 2048 to 4095, ...) at most 96 rows name the same one
- symbol_lane: int32 [65536], P(('tm', 'sym')), may hold values from 0 to 15
- quote_offset: int32 [65536], P(('tm', 'sym')), may hold values from 0 to 511
- quotes: float32 [64, 4096, 128], P('sym', 'tm'), may hold values from -6 to 6
- rates: float32 [128], replicated, may hold values from 0.05 to 2
Outputs:
- joined: float32 [65536, 128], P(('tm', 'sym'))
Inputs may be any that keep to these rules, and one draw needn't show every extreme that they name: Among the 2048 trades of one device no owner is named more than 96 times, and in every draw some device names some owner exactly 96 times. Owner o holds symbols of group o % 4 and quote rows of block o // 4.
All inputs are finite; a program needn't handle non-finite values.
Results may differ from a plain program's by a relative error of at most 0.00002.
Values sent between devices are 32-bit elements; how exact they have to be, the bound alone decides.
A program may use at most 64 MiB of HBM per device.

v0:
```python
import jax
import jax.numpy as jnp
from jax import lax
from jax.sharding import PartitionSpec as P


def passed_along(block, axis, distance):
    devices = range(lax.axis_size(axis))
    route = [(i - distance, i) for i in devices if i - distance in devices]
    return lax.ppermute(block, axis, route)


def ranks_of(destination):
    tick_count = destination.shape[0]
    block_rows = min(512, tick_count)
    positions = jnp.arange(tick_count, dtype=jnp.int32)

    def one_block(start):
        block_dest = lax.dynamic_slice_in_dim(destination, start, block_rows)
        block_pos = start + jnp.arange(block_rows, dtype=jnp.int32)
        same_owner = (block_dest[:, None] == destination[None, :]) & (
            positions[None, :] < block_pos[:, None]
        )
        return jnp.sum(same_owner.astype(jnp.int32), axis=1)

    block_starts = jnp.arange(tick_count // block_rows, dtype=jnp.int32) * block_rows
    return lax.map(one_block, block_starts).reshape(tick_count)


def per_device(trade_age, trade_size, owner, symbol_lane, quote_offset, quotes, rates):
    time_shards = lax.axis_size("tm")
    symbol_shards = lax.axis_size("sym")
    device_count = time_shards * symbol_shards
    tick_count = trade_age.shape[0]
    capacity = 3 * tick_count // (2 * device_count)
    lane_count = quotes.shape[0]
    quote_rows = quotes.shape[1]
    features = quotes.shape[2]
    slot_count = device_count * capacity
    boundary = passed_along(quotes[:, quote_rows - 1, :], "tm", 1)
    destination = owner[:, 0]
    slot = destination * capacity + ranks_of(destination)
    local_row = symbol_lane * quote_rows + quote_offset
    packed = jnp.stack([local_row.astype(jnp.float32), trade_age, trade_size], axis=0)
    send_block = jnp.zeros((3, slot_count), jnp.float32).at[:, slot].set(packed)
    arrived = lax.all_to_all(send_block, ("tm", "sym"), split_axis=1, concat_axis=1, tiled=True)
    got_rows = arrived[0].astype(jnp.int32)
    got_ages = arrived[1]
    got_sizes = arrived[2]
    flat_count = lane_count * quote_rows
    table = jnp.concatenate([quotes.reshape(flat_count, features), boundary], axis=0)
    lane_index = got_rows // quote_rows
    row_offset = got_rows % quote_rows
    prior_index = jnp.where(row_offset == 0, flat_count + lane_index, got_rows - 1)
    current = table[got_rows]
    previous = table[prior_index]
    weight = jnp.exp(-got_ages[:, None] * rates[None, :])
    joined = got_sizes[:, None] * (weight * current + (1.0 - weight) * previous)
    returned = lax.all_to_all(joined, ("tm", "sym"), split_axis=0, concat_axis=0, tiled=True)
    return returned[slot]


def solution(mesh):
    in_specs = (
        P(("tm", "sym")),
        P(("tm", "sym")),
        P(("tm", "sym"), None),
        P(("tm", "sym")),
        P(("tm", "sym")),
        P("sym", "tm", None),
        P(),
    )
    out_specs = P(("tm", "sym"), None)
    return jax.shard_map(
        per_device, mesh=mesh, in_specs=in_specs, out_specs=out_specs, check_vma=False
    )
```

profile of v0, /device:TPU:0, one launch (start us, length us, event | category | flops | bytes accessed | tf_op | source)
XLA Modules:
  0.0 121.3 jit_solution(11804871727491754775)
XLA Ops:
  0.0 0.8 slice.17
  0.8 4.9 %collective-permute-start = (f32[16,128]{1,0:T(8,128)S(1)}, f32[16,128]{1,0:T(8,128)S(1)}, u32[]{:S(2)}, u32[]{:S(2)}) collective-permute-start(f32[16,128]{1,0:T(8,128)S(1)} %bitcast.57), channel_id=1, source_target_pairs={{0,4},{4,8},{8,12},{12,16},{16,20},{20,24},{24,28},{1,5},{5,9},{9,... | collective-permute-start | bytes 24584 | tf_op jit(solution)/shard_map/ppermute | solution.py:10
  5.8 22.7 %while.11 = (s32[]{:T(128)}, s32[4,512]{1,0:T(4,128)S(1)}, s32[4]{0:T(128)S(1)}, s32[2048]{0:T(1024)}, s32[2048,1]{0,1:T(1,128)}, /*index=5*/s32[]{:T(128)}, s32[]{:T(128)}, s32[]{:T(128)}) while((s32[]{:T(128)}, s32[4,512]{1,0:T(4,128)S(1)}, s32[4]{0:T(128)S(1)}, s32[2048]{0:T(1024)}, s32[2048,1]{0,1:T(1,128)}, ...), condition=%wide.region_2.3_spmd.clone, body=%wide.region_0.2_spmd.clone.sunk | while | flops 5242885 | bytes 24727 | solution.py:27
  5.8 0.6 dynamic_slice.11
  8.3 0.8 dynamic_slice.12
  9.1 0.6 iota_add_fusion.2
  9.7 1.7 %convert_reduce_fusion.2 = s32[512]{0:T(512)S(1)} fusion(s32[512]{0:T(512)S(1)} %iota_add_fusion.2, s32[2048]{0:T(1024)} %bitcast.49, s32[512]{0:T(512)S(1)} %dynamic_slice.12), kind=kLoop, calls=%fused_computation.6.clone.1 | loop fusion | flops 5242368 | bytes 14336 | tf_op jit(solution)/shard_map/while/body/eval_jaxpr/reduce_sum | solution.py:24
  11.4 0.6 dynamic_slice.11
  14.0 0.8 dynamic_slice.12
  14.7 0.6 iota_add_fusion.2
  15.4 1.7 %convert_reduce_fusion.2 = s32[512]{0:T(512)S(1)} fusion(s32[512]{0:T(512)S(1)} %iota_add_fusion.2, s32[2048]{0:T(1024)} %bitcast.49, s32[512]{0:T(512)S(1)} %dynamic_slice.12), kind=kLoop, calls=%fused_computation.6.clone.1 | loop fusion | flops 5242368 | bytes 14336 | tf_op jit(solution)/shard_map/while/body/eval_jaxpr/reduce_sum | solution.py:24
  17.1 0.6 dynamic_slice.11
  19.6 0.8 dynamic_slice.12
  20.4 0.6 iota_add_fusion.2
  21.0 1.7 %convert_reduce_fusion.2 = s32[512]{0:T(512)S(1)} fusion(s32[512]{0:T(512)S(1)} %iota_add_fusion.2, s32[2048]{0:T(1024)} %bitcast.49, s32[512]{0:T(512)S(1)} %dynamic_slice.12), kind=kLoop, calls=%fused_computation.6.clone.1 | loop fusion | flops 5242368 | bytes 14336 | tf_op jit(solution)/shard_map/while/body/eval_jaxpr/reduce_sum | solution.py:24
  25.3 0.8 dynamic_slice.12
  26.1 0.6 iota_add_fusion.2
  26.7 1.7 %convert_reduce_fusion.2 = s32[512]{0:T(512)S(1)} fusion(s32[512]{0:T(512)S(1)} %iota_add_fusion.2, s32[2048]{0:T(1024)} %bitcast.49, s32[512]{0:T(512)S(1)} %dynamic_slice.12), kind=kLoop, calls=%fused_computation.6.clone.1 | loop fusion | flops 5242368 | bytes 14336 | tf_op jit(solution)/shard_map/while/body/eval_jaxpr/reduce_sum | solution.py:24
  28.4 0.7 compare_select_fusion.2
  29.2 0.7 add_convert_fusion
  29.9 0.7 maximum_bitcast_fusion
  31.0 6.0 %scatter_custom_fusion = f32[3,3072]{0,1:T(8,128)S(1)} fusion(s32[2048]{0:T(1024)S(1)} %bitcast.52, f32[2048,3]{1,0:T(8,128)S(1)} %copy.17, f32[]{:T(128)} %constant.29.clone.1), kind=kCustom, calls=%fused_computation.11 | custom fusion | bytes 36868 | tf_op jit(solution)/shard_map/scatter | solution.py:45
  37.0 1.1 copy.18
  38.1 4.9 %all-to-all-start = ((f32[3,32,96]{2,0,1:T(4,128)}), f32[3,32,96]{2,0,1:T(4,128)S(1)}, u32[]{:S(2)}, u32[]{:S(2)}) async-start(f32[3,32,96]{2,0,1:T(4,128)} %copy.18), calls=%async_computation | async-start | bytes 131072 | tf_op jit(solution)/shard_map/all_to_all | solution.py:46
  43.0 4.3 %pad_maximum_fusion = f32[8208,128]{1,0:T(8,128)} fusion(f32[16,128]{1,0:T(8,128)S(1)} %collective-permute-done, f32[8192,128]{1,0:T(8,128)} %bitcast.41), kind=kLoop, calls=%fused_computation.9 | loop fusion | flops 1050624 | bytes 8404992 | tf_op jit(solution)/shard_map/concatenate | solution.py:51
  47.3 3.1 %all-to-all-done = f32[3,32,96]{2,0,1:T(4,128)S(1)} async-done(((f32[3,32,96]{2,0,1:T(4,128)}), f32[3,32,96]{2,0,1:T(4,128)S(1)}, u32[]{:S(2)}, u32[]{:S(2)}) %all-to-all-start) | async-done | bytes 36896 | tf_op jit(solution)/shard_map/all_to_all | solution.py:46
  50.8 10.3 %gather_fusion.1 = f32[3072,128]{1,0:T(8,128)S(1)} fusion(f32[8208,128]{1,0:T(8,128)} %pad_maximum_fusion, s32[3072]{0:T(1024)S(1)} %broadcast_clamp_fusion), kind=kCustom, calls=%fused_computation.1 | custom fusion | bytes 3158016 | tf_op jit(solution)/shard_map/gather | solution.py:56
  61.1 10.3 %gather_fusion = f32[3072,128]{1,0:T(8,128)S(1)} fusion(f32[8208,128]{1,0:T(8,128)} %pad_maximum_fusion, s32[3072]{0:T(1024)S(1)} %broadcast_clamp_fusion.1), kind=kCustom, calls=%fused_computation | custom fusion | bytes 3158016 | tf_op jit(solution)/shard_map/gather | solution.py:55
  71.5 1.9 %add_multiply_fusion = f32[32,96,128]{2,1,0:T(8,128)} fusion(f32[32,96,128]{2,1,0:T(8,128)S(1)} %bitcast.38, f32[32,96,128]{2,1,0:T(8,128)S(1)} %bitcast.39, f32[128]{0:T(128)S(1)} %copy-done, f32[32,96]{1,0:T(8,128)S(1)} %negate_bitcast_fusion, f32[32,96]{1,0:T(8,128)S(1)} %bitcast.42), kind=kLoop, calls=%fused_computation.10 | loop fusion | flops 2359296 | bytes 4743680 | tf_op jit(solution)/shard_map/mul | solution.py:58
  73.3 2.7 %all-to-all-start.1 = ((f32[32,96,128]{2,1,0:T(8,128)}), f32[32,96,128]{2,1,0:T(8,128)S(1)}, u32[]{:S(2)}, u32[]{:S(2)}) async-start(f32[32,96,128]{2,1,0:T(8,128)} %add_multiply_fusion), calls=%async_computation.1 | async-start | bytes 3145728 | tf_op jit(solution)/shard_map/all_to_all | solution.py:59
  76.1 37.6 %all-to-all-done.1 = f32[32,96,128]{2,1,0:T(8,128)S(1)} async-done(((f32[32,96,128]{2,1,0:T(8,128)}), f32[32,96,128]{2,1,0:T(8,128)S(1)}, u32[]{:S(2)}, u32[]{:S(2)}) %all-to-all-start.1) | async-done | bytes 1572896 | tf_op jit(solution)/shard_map/all_to_all | solution.py:59
  113.7 7.6 %gather_fusion.2 = f32[2048,128]{1,0:T(8,128)} fusion(f32[3072,128]{1,0:T(8,128)S(1)} %bitcast.37, s32[2048]{0:T(1024)S(1)} %broadcast_clamp_fusion.2), kind=kCustom, calls=%fused_computation.2 | custom fusion | bytes 2105344 | tf_op jit(solution)/shard_map/gather | solution.py:60
  (20 shorter events, 1.5 us)
Async XLA Ops:
  0.8 42.2 %collective-permute-start = (f32[16,128]{1,0:T(8,128)S(1)}, f32[16,128]{1,0:T(8,128)S(1)}, u32[]{:S(2)}, u32[]{:S(2)}) collective-permute-start(f32[16,128]{1,0:T(8,128)S(1)} %bitcast.57), channel_id=1, source_target_pairs={{0,4},{4,8},{8,12},{12,16},{16,20},{20,24},{24,28},{1,5},{5,9},{9,... | collective-permute-start | bytes 24584 | tf_op jit(solution)/shard_map/ppermute | solution.py:10
  38.1 12.3 %all-to-all-start = ((f32[3,32,96]{2,0,1:T(4,128)}), f32[3,32,96]{2,0,1:T(4,128)S(1)}, u32[]{:S(2)}, u32[]{:S(2)}) async-start(f32[3,32,96]{2,0,1:T(4,128)} %copy.18), calls=%async_computation | async-start | bytes 131072 | tf_op jit(solution)/shard_map/all_to_all | solution.py:46
  61.1 10.3 %copy-start = (f32[128]{0:T(128)S(1)}, f32[128]{0:T(128)}, u32[]{:S(2)}) copy-start(f32[128]{0:T(128)} %param.15) | copy-start | bytes 1540
  73.3 40.4 %all-to-all-start.1 = ((f32[32,96,128]{2,1,0:T(8,128)}), f32[32,96,128]{2,1,0:T(8,128)S(1)}, u32[]{:S(2)}, u32[]{:S(2)}) async-start(f32[32,96,128]{2,1,0:T(8,128)} %add_multiply_fusion), calls=%async_computation.1 | async-start | bytes 3145728 | tf_op jit(solution)/shard_map/all_to_all | solution.py:59
where the time goes:
time: 122 us; the launch traced here: 121 us
  local copies, waits for them, and re-layouts  42.4 us (35%)
  waiting for transfers between devices  40.7 us (33%)
  other arithmetic  17.7 us (15%)
  starting transfers between devices  12.5 us (10%)
  loops' own time  7.74 us (6%)
    all_to_all x1, waiting for transfers between devices, per_device(): lax.all_to_all(joined, ('tm', 'sym'), split_axis=0, concat_axis=0, tiled=...  37.6 us
    gather x1, local copies, waits for them, and re-layouts, per_device(): current = table[got_rows]  10.3 us
    gather x1, local copies, waits for them, and re-layouts, per_device(): previous = table[prior_index]  10.3 us
    another operation x1, loops' own time, ranks_of(): return lax.map(one_block, block_starts).reshape(tick_count)  7.74 us
    gather x1, local copies, waits for them, and re-layouts, per_device(): return returned[slot]  7.63 us
    reduce_sum x4, other arithmetic, one_block(): return jnp.sum(same_owner.astype(jnp.int32), axis=1)  6.66 us
    scatter x1, local copies, waits for them, and re-layouts, per_device(): send_block = jnp.zeros((3, slot_count), jnp.float32).at[:, slot].set(packed)  5.99 us
    all_to_all x1, starting transfers between devices, per_device(): lax.all_to_all(send_block, ('tm', 'sym'), split_axis=1, concat_axis=1, ti...  4.9 us
  transfers between devices with their start and end apart: 3, of which 2 were waited for; matrix products, arithmetic and copies ran while one was open for 24% of the time, Pallas kernels for 0%

commit v1 on v0

v1 whole, which is shorter than its diff:
```python
import functools

import jax
import jax.numpy as jnp
from jax import lax
from jax.experimental import pallas as pl
from jax.experimental.pallas import tpu as pltpu
from jax.sharding import PartitionSpec as P

LANES = 128
PAD = 8
MESH = pl.DeviceIdType.MESH


def partner(me, k, devices):
    if devices & (devices - 1):
        return (me + k) % devices
    out, bit = 0, 1
    while bit < devices:
        out = out + ((me // bit) % 2 + (k // bit) % 2) % 2 * bit
        bit *= 2
    return out


def join_kernel(
    cfg,
    owner_ref, lane_ref, offset_ref, age_ref, rates_ref, quotes_ref,
    out_ref,
    table, recv, sbuf, msg, got, rows_v, rows_s, slot_v, slot_s, cur, prev, bsend, brecv,
    qsem, bsem, msend, mrecv, jsend, jrecv, ssem,
):
    tm_n, sym_n, cap = cfg
    devices = tm_n * sym_n
    ticks = owner_ref.shape[1]
    lane_count, quote_rows, features = quotes_ref.shape
    stride = quote_rows + PAD
    tm, sym = lax.axis_index("tm"), lax.axis_index("sym")
    me = tm * sym_n + sym

    def device(p):
        return (p // sym_n, p % sym_n)

    loads = [
        pltpu.make_async_copy(
            quotes_ref.at[lane], table.at[pl.ds(lane * stride + PAD, quote_rows)], qsem.at[lane]
        )
        for lane in range(lane_count)
    ]
    for load in loads:
        load.start()

    barrier = pltpu.get_barrier_semaphore()

    @pl.loop(1, devices)
    def _(k):
        pl.semaphore_signal(
            barrier, inc=1, device_id=device(partner(me, k, devices)), device_id_type=MESH
        )

    owner = owner_ref[...]
    mine = owner == lax.broadcasted_iota(jnp.int32, (devices, ticks), 0)
    hot = mine.astype(jnp.float32)
    hot_b = hot.astype(jnp.bfloat16)
    width = 256 if ticks % 256 == 0 else 128
    upper = (
        lax.broadcasted_iota(jnp.int32, (width, width), 0)
        < lax.broadcasted_iota(jnp.int32, (width, width), 1)
    ).astype(jnp.float32).astype(jnp.bfloat16)
    base = jnp.zeros((devices, 1), jnp.float32)
    ranks = []
    for start in range(0, ticks, width):
        part = hot[:, start:start + width]
        before = jnp.dot(
            hot_b[:, start:start + width], upper, preferred_element_type=jnp.float32
        )
        ranks.append(jnp.sum(part * (before + base), axis=0, keepdims=True))
        base = base + jnp.sum(part, axis=1, keepdims=True)
    rank = jnp.concatenate(ranks, axis=1)
    slot_v[...] = jnp.clip(owner * cap + rank.astype(jnp.int32), 0, devices * cap - 1)
    slot_copy = pltpu.make_async_copy(slot_v, slot_s, ssem.at[0])
    slot_copy.start()

    place = (
        rank.astype(jnp.int32) == lax.broadcasted_iota(jnp.int32, (LANES, ticks), 0)
    ).astype(jnp.float32).astype(jnp.bfloat16)
    local = lane_ref[...] * stride + PAD - 1 + offset_ref[...]
    age = age_ref[...]
    high = age.astype(jnp.bfloat16).astype(jnp.float32)
    middle = (age - high).astype(jnp.bfloat16).astype(jnp.float32)
    low = age - high - middle
    pieces = [
        (local // LANES).astype(jnp.float32), (local % LANES).astype(jnp.float32), high, middle, low
    ]
    spread = jnp.concatenate([(hot * piece).astype(jnp.bfloat16) for piece in pieces], axis=0)
    put = lax.dot_general(
        spread, place, (((1,), (1,)), ((), ())), preferred_element_type=jnp.float32
    )
    taken = [put[i * devices:(i + 1) * devices] for i in range(5)]
    msg[:, 0, 0:LANES] = taken[0] * LANES + taken[1]
    msg[:, 0, LANES:2 * LANES] = (taken[2] + taken[3]) + taken[4]

    for load in loads:
        load.wait()
    for lane in range(lane_count):
        bsend[lane:lane + 1, :] = table[(lane + 1) * stride - 1:(lane + 1) * stride, :]
    pl.semaphore_wait(barrier, devices - 1)

    def boundary():
        return pltpu.make_async_remote_copy(
            src_ref=bsend, dst_ref=brecv, send_sem=bsem.at[0], recv_sem=bsem.at[1],
            device_id=(lax.rem(tm + 1, tm_n), sym), device_id_type=MESH,
        )

    @pl.when(tm < tm_n - 1)
    def _():
        boundary().start()

    def message(p):
        return pltpu.make_async_remote_copy(
            src_ref=msg.at[p], dst_ref=got.at[me], send_sem=msend.at[p], recv_sem=mrecv.at[me],
            device_id=device(p), device_id_type=MESH,
        )

    def message_in(p):
        return pltpu.make_async_remote_copy(
            src_ref=msg.at[p], dst_ref=got.at[p], send_sem=msend.at[p], recv_sem=mrecv.at[p],
            device_id=device(p), device_id_type=MESH,
        )

    @pl.loop(1, devices)
    def _(k):
        message(partner(me, devices - k, devices)).start()

    got[me] = msg[me]

    @pl.loop(1, devices)
    def _(k):
        message_in(partner(me, devices - k, devices)).wait_recv()

    rows_v[...] = jnp.clip(got[:, :, 0:LANES].astype(jnp.int32), 0, lane_count * stride - 2)
    rows_copy = pltpu.make_async_copy(rows_v, rows_s, ssem.at[1])
    rows_copy.start()

    @pl.when(tm > 0)
    def _():
        boundary().wait_recv()

    @pl.when(tm == 0)
    def _():
        brecv[...] = jnp.zeros_like(brecv)

    edge = brecv[...]
    for lane in range(lane_count):
        table[lane * stride + PAD - 1:lane * stride + PAD, :] = edge[lane:lane + 1, :]
    rows_copy.wait()

    rates = rates_ref[...]

    def joined(p):
        for r in range(cap):
            row = rows_s[p, 0, r]
            cur[r:r + 1, :] = table[pl.ds(row + 1, 1), :]
            prev[r:r + 1, :] = table[pl.ds(row, 1), :]
        ages = got[p, :, LANES:2 * LANES]
        ages = jnp.transpose(jnp.broadcast_to(ages, (LANES, LANES)))[:cap]
        weight = jnp.exp(-ages * rates)
        return weight * cur[...] + (1.0 - weight) * prev[...]

    def share(p, source):
        return pltpu.make_async_remote_copy(
            src_ref=sbuf.at[p],
            dst_ref=recv.at[pl.ds(pl.multiple_of(source * cap, 8), cap)],
            send_sem=jsend.at[p], recv_sem=jrecv.at[source],
            device_id=device(p), device_id_type=MESH,
        )

    @pl.loop(1, devices)
    def _(k):
        p = partner(me, devices - k, devices)
        sbuf[p] = joined(p)
        share(p, me).start()

    recv[pl.ds(pl.multiple_of(me * cap, 8), cap), :] = joined(me)
    slot_copy.wait()

    @pl.when(tm < tm_n - 1)
    def _():
        boundary().wait_send()

    @pl.loop(1, devices)
    def _(k):
        p = partner(me, devices - k, devices)
        message(p).wait_send()
        share(p, p).wait_recv()

    unroll = 32

    @pl.loop(0, ticks // unroll)
    def _(b):
        start = pl.multiple_of(b * unroll, unroll)
        for u in range(unroll):
            out_ref[pl.ds(start + u, 1), :] = recv[pl.ds(slot_s[0, start + u], 1), :]

    @pl.loop(1, devices)
    def _(k):
        share(partner(me, devices - k, devices), me).wait_send()


def per_device(trade_age, trade_size, owner, symbol_lane, quote_offset, quotes, rates):
    tm_n, sym_n = lax.axis_size("tm"), lax.axis_size("sym")
    devices = tm_n * sym_n
    ticks = trade_age.shape[0]
    cap = 3 * ticks // (2 * devices)
    lane_count, quote_rows, features = quotes.shape
    vmem = pl.BlockSpec(memory_space=pltpu.VMEM)
    dma = pltpu.SemaphoreType.DMA
    joined = pl.pallas_call(
        functools.partial(join_kernel, (tm_n, sym_n, cap)),
        out_shape=jax.ShapeDtypeStruct((ticks, features), jnp.float32),
        in_specs=[vmem] * 5 + [pl.BlockSpec(memory_space=pl.ANY)],
        out_specs=vmem,
        scratch_shapes=[
            pltpu.VMEM((lane_count * (quote_rows + PAD), features), jnp.float32),
            pltpu.VMEM((devices * cap, features), jnp.float32),
            pltpu.VMEM((devices, cap, features), jnp.float32),
            pltpu.VMEM((devices, 1, 2 * LANES), jnp.float32),
            pltpu.VMEM((devices, 1, 2 * LANES), jnp.float32),
            pltpu.VMEM((devices, 1, LANES), jnp.int32),
            pltpu.SMEM((devices, 1, LANES), jnp.int32),
            pltpu.VMEM((1, ticks), jnp.int32),
            pltpu.SMEM((1, ticks), jnp.int32),
            pltpu.VMEM((cap, features), jnp.float32),
            pltpu.VMEM((cap, features), jnp.float32),
            pltpu.VMEM((lane_count, features), jnp.float32),
            pltpu.VMEM((lane_count, features), jnp.float32),
            dma((lane_count,)), dma((2,)),
            dma((devices,)), dma((devices,)), dma((devices,)), dma((devices,)),
            dma((2,)),
        ],
        compiler_params=pltpu.CompilerParams(collective_id=0, has_side_effects=True),
    )(
        owner.reshape(1, ticks), symbol_lane.reshape(1, ticks), quote_offset.reshape(1, ticks),
        trade_age.reshape(1, ticks), rates.reshape(1, features), quotes,
    )
    return trade_size[:, None] * joined


def solution(mesh):
    in_specs = (
        P(("tm", "sym")),
        P(("tm", "sym")),
        P(("tm", "sym"), None),
        P(("tm", "sym")),
        P(("tm", "sym")),
        P("sym", "tm", None),
        P(),
    )
    out_specs = P(("tm", "sym"), None)
    return jax.shard_map(
        per_device, mesh=mesh, in_specs=in_specs, out_specs=out_specs, check_vma=False
    )
```

time: 122 us -> 61.2 us (0.50)
  Pallas kernels: 0 us -> 58.4 us
  local copies, waits for them, and re-layouts: 42.4 us -> 0.01 us
  waiting for transfers between devices: 40.7 us -> 0 us
  other arithmetic: 17.7 us -> 2.53 us
  starting transfers between devices: 12.5 us -> 0 us
  loops' own time: 7.74 us -> 0 us
    pallas_call x0 -> x1, Pallas kernels: none -> 58.4 us  [per_device(): pl.pallas_call(functools.partial(join_kernel, (tm_n, sym_n, cap)), out_sh...]
    all_to_all x2 -> x0, waiting for transfers between devices: 40.7 us -> none  [the longest x1 37.6 us: per_device(): lax.all_to_all(joined, ('tm', 'sym'), split_axis=0, concat_axis=0, tiled=...]
    gather x3 -> x0, local copies, waits for them, and re-layouts: 28.3 us -> none  [the longest x1 10.3 us: per_device(): current = table[got_rows]]
    another operation x1 -> x0, loops' own time: 7.74 us -> none  [ranks_of(): return lax.map(one_block, block_starts).reshape(tick_count)]
    all_to_all x2 -> x0, starting transfers between devices: 7.62 us -> none  [the longest x1 4.9 us: per_device(): lax.all_to_all(send_block, ('tm', 'sym'), split_axis=1, concat_axis=1, ti...]
    reduce_sum x4 -> x0, other arithmetic: 6.66 us -> none  [one_block(): return jnp.sum(same_owner.astype(jnp.int32), axis=1)]
    scatter x1 -> x0, local copies, waits for them, and re-layouts: 5.99 us -> none  [per_device(): send_block = jnp.zeros((3, slot_count), jnp.float32).at[:, slot].set(packed)]
    dynamic_slice x8 -> x0, local copies, waits for them, and re-layouts: 5.54 us -> none  [the longest x4 3.09 us: one_block(): block_dest = lax.dynamic_slice_in_dim(destination, start, block_rows)]
  transfers between devices with their start and end apart: 3 -> 0, of which waited for: 2 -> 0; matrix products, arithmetic and copies ran while one was open for 24% -> 0% of each run, Pallas kernels for 0% -> 0%
where the time goes in v1:
time: 61.2 us; the launch traced here: 61 us
  Pallas kernels  58.4 us (95%)
  other arithmetic  2.53 us (4%)
    pallas_call x1, Pallas kernels, per_device(): pl.pallas_call(functools.partial(join_kernel, (tm_n, sym_n, cap)), out_sh...  58.4 us
    mul x1, other arithmetic, per_device(): return trade_size[:, None] * joined  2.53 us

profile of v1, /device:TPU:0, one launch (start us, length us, event | category | flops | bytes accessed | tf_op | source)
XLA Modules:
  0.0 61.0 jit_solution(6857604910562522755)
XLA Ops:
  0.0 0.0 copy-start
  0.0 58.4 %shard_map.73 = f32[2048,128]{1,0:T(8,128)} custom-call(s32[1,2048]{1,0:T(1,128)} %bitcast.5, s32[1,2048]{1,0:T(1,128)} %bitcast.6, s32[1,2048]{1,0:T(1,128)} %bitcast.7, f32[1,2048]{1,0:T(1,128)} %bitcast.8, f32[1,128]{1,0:T(1,128)} %bitcast.9, f32[16,512,128]{2,1,0:T(8,128)} %quotes_ref.1), custom_call_target="tpu_custom_call" | custom-call | tf_op jit(solution)/shard_map/pallas_call | solution.py:217
  58.4 0.0 copy-done
  58.4 2.5 %broadcast_multiply_fusion = f32[2048,128]{1,0:T(8,128)} fusion(f32[2048,128]{1,0:T(8,128)} %shard_map.73, f32[2048]{0:T(1024)S(1)} %copy-done), kind=kLoop, calls=%fused_computation | loop fusion | flops 262144 | bytes 2105344 | tf_op jit(solution)/shard_map/mul | solution.py:245
Async XLA Ops:
  0.0 58.4 %copy-start = (f32[2048]{0:T(1024)S(1)}, f32[2048]{0:T(1024)}, u32[]{:S(2)}) copy-start(f32[2048]{0:T(1024)} %param.8) | copy-start | bytes 24580

commit v2 on v1

--- a/solution.py
+++ b/solution.py
@@ -12,12 +12,10 @@
 MESH = pl.DeviceIdType.MESH
 
 
-def partner(me, k, devices):
-    if devices & (devices - 1):
-        return (me + k) % devices
-    out, bit = 0, 1
+def flips(me, devices):
+    out, bit = [], 1
     while bit < devices:
-        out = out + ((me // bit) % 2 + (k // bit) % 2) % 2 * bit
+        out.append(bit - 2 * bit * lax.rem(lax.div(me, bit), 2))
         bit *= 2
     return out
 
@@ -37,8 +35,20 @@
     tm, sym = lax.axis_index("tm"), lax.axis_index("sym")
     me = tm * sym_n + sym
 
+    flip = flips(me, devices)
+    group = min(8, devices)
+
+    def peer(k):
+        p = me
+        for i, step in enumerate(flip):
+            if k >> i & 1:
+                p = p + step
+        return p
+
     def device(p):
-        return (p // sym_n, p % sym_n)
+        return (lax.div(p, sym_n), lax.rem(p, sym_n))
+
+    everyone = range(devices - 1, 0, -1)
 
     loads = [
         pltpu.make_async_copy(
@@ -51,11 +61,8 @@
 
     barrier = pltpu.get_barrier_semaphore()
 
-    @pl.loop(1, devices)
-    def _(k):
-        pl.semaphore_signal(
-            barrier, inc=1, device_id=device(partner(me, k, devices)), device_id_type=MESH
-        )
+    for k in everyone:
+        pl.semaphore_signal(barrier, inc=1, device_id=device(peer(k)), device_id_type=MESH)
 
     owner = owner_ref[...]
     mine = owner == lax.broadcasted_iota(jnp.int32, (devices, ticks), 0)
@@ -99,11 +106,27 @@
     msg[:, 0, 0:LANES] = taken[0] * LANES + taken[1]
     msg[:, 0, LANES:2 * LANES] = (taken[2] + taken[3]) + taken[4]
 
+    def message(p):
+        return pltpu.make_async_remote_copy(
+            src_ref=msg.at[p], dst_ref=got.at[me], send_sem=msend.at[p], recv_sem=mrecv.at[me],
+            device_id=device(p), device_id_type=MESH,
+        )
+
+    def message_in(p):
+        return pltpu.make_async_remote_copy(
+            src_ref=msg.at[p], dst_ref=got.at[p], send_sem=msend.at[p], recv_sem=mrecv.at[p],
+            device_id=device(p), device_id_type=MESH,
+        )
+
+    pl.semaphore_wait(barrier, devices - 1)
+    for k in everyone:
+        message(peer(k)).start()
+    got[me] = msg[me]
+
     for load in loads:
         load.wait()
     for lane in range(lane_count):
         bsend[lane:lane + 1, :] = table[(lane + 1) * stride - 1:(lane + 1) * stride, :]
-    pl.semaphore_wait(barrier, devices - 1)
 
     def boundary():
         return pltpu.make_async_remote_copy(
@@ -115,44 +138,17 @@
     def _():
         boundary().start()
 
-    def message(p):
-        return pltpu.make_async_remote_copy(
-            src_ref=msg.at[p], dst_ref=got.at[me], send_sem=msend.at[p], recv_sem=mrecv.at[me],
-            device_id=device(p), device_id_type=MESH,
-        )
-
-    def message_in(p):
-        return pltpu.make_async_remote_copy(
-            src_ref=msg.at[p], dst_ref=got.at[p], send_sem=msend.at[p], recv_sem=mrecv.at[p],
-            device_id=device(p), device_id_type=MESH,
-        )
-
-    @pl.loop(1, devices)
-    def _(k):
-        message(partner(me, devices - k, devices)).start()
-
-    got[me] = msg[me]
-
-    @pl.loop(1, devices)
-    def _(k):
-        message_in(partner(me, devices - k, devices)).wait_recv()
-
-    rows_v[...] = jnp.clip(got[:, :, 0:LANES].astype(jnp.int32), 0, lane_count * stride - 2)
-    rows_copy = pltpu.make_async_copy(rows_v, rows_s, ssem.at[1])
-    rows_copy.start()
+    @pl.when(tm == 0)
+    def _():
+        brecv[...] = jnp.zeros_like(brecv)
 
     @pl.when(tm > 0)
     def _():
         boundary().wait_recv()
-
-    @pl.when(tm == 0)
-    def _():
-        brecv[...] = jnp.zeros_like(brecv)
 
     edge = brecv[...]
     for lane in range(lane_count):
         table[lane * stride + PAD - 1:lane * stride + PAD, :] = edge[lane:lane + 1, :]
-    rows_copy.wait()
 
     rates = rates_ref[...]
 
@@ -174,11 +170,27 @@
             device_id=device(p), device_id_type=MESH,
         )
 
-    @pl.loop(1, devices)
-    def _(k):
-        p = partner(me, devices - k, devices)
-        sbuf[p] = joined(p)
-        share(p, me).start()
+    for g in range(devices // group - 1, -1, -1):
+        lead = peer(g * group)
+        for j in range(group - 1, -1, -1):
+            if g or j:
+                message_in(peer(g * group + j)).wait_recv()
+        whole = pl.ds(pl.multiple_of(lax.div(lead, group) * group, group), group)
+        rows_v[whole] = jnp.clip(
+            got[whole, :, 0:LANES].astype(jnp.int32), 0, lane_count * stride - 2
+        )
+        rows_copy = pltpu.make_async_copy(rows_v.at[whole], rows_s.at[whole], ssem.at[1])
+        rows_copy.start()
+        rows_copy.wait()
+
+        @pl.loop(0 if g else 1, group)
+        def _(j, lead=lead):
+            p, bit = lead, 1
+            for step in flip[:group.bit_length() - 1]:
+                p = p + lax.rem(lax.div(j, bit), 2) * step
+                bit *= 2
+            sbuf[p] = joined(p)
+            share(p, me).start()
 
     recv[pl.ds(pl.multiple_of(me * cap, 8), cap), :] = joined(me)
     slot_copy.wait()
@@ -187,11 +199,10 @@
     def _():
         boundary().wait_send()
 
-    @pl.loop(1, devices)
-    def _(k):
-        p = partner(me, devices - k, devices)
-        message(p).wait_send()
-        share(p, p).wait_recv()
+    for k in everyone:
+        message(peer(k)).wait_send()
+    for k in everyone:
+        share(peer(k), peer(k)).wait_recv()
 
     unroll = 32
 
@@ -201,9 +212,8 @@
         for u in range(unroll):
             out_ref[pl.ds(start + u, 1), :] = recv[pl.ds(slot_s[0, start + u], 1), :]
 
-    @pl.loop(1, devices)
-    def _(k):
-        share(partner(me, devices - k, devices), me).wait_send()
+    for k in everyone:
+        share(peer(k), me).wait_send()
 
 
 def per_device(trade_age, trade_size, owner, symbol_lane, quote_offset, quotes, rates):
@@ -217,7 +227,7 @@
     joined = pl.pallas_call(
         functools.partial(join_kernel, (tm_n, sym_n, cap)),
         out_shape=jax.ShapeDtypeStruct((ticks, features), jnp.float32),
-        in_specs=[vmem] * 5 + [pl.BlockSpec(memory_space=pl.ANY)],
+        in_specs=[vmem] * 5 + [pl.BlockSpec(memory_space=pltpu.HBM)],
         out_specs=vmem,
         scratch_shapes=[
             pltpu.VMEM((lane_count * (quote_rows + PAD), features), jnp.float32),
@@ -237,7 +247,9 @@
             dma((devices,)), dma((devices,)), dma((devices,)), dma((devices,)),
             dma((2,)),
         ],
-        compiler_params=pltpu.CompilerParams(collective_id=0, has_side_effects=True),
+        compiler_params=pltpu.CompilerParams(
+            collective_id=0, has_side_effects=True, vmem_limit_bytes=60 << 20
+        ),
     )(
         owner.reshape(1, ticks), symbol_lane.reshape(1, ticks), quote_offset.reshape(1, ticks),
         trade_age.reshape(1, ticks), rates.reshape(1, features), quotes,

time: 61.2 us -> 56.7 us (0.926)
  Pallas kernels: 58.4 us -> 54 us
    pallas_call x1, Pallas kernels: 58.4 us -> 54 us  [per_device(): pl.pallas_call(functools.partial(join_kernel, (tm_n, sym_n, cap)), out_sh...]
where the time goes in v2:
time: 56.7 us; the launch traced here: 56.5 us
  Pallas kernels  54 us (95%)
  other arithmetic  2.53 us (4%)
    pallas_call x1, Pallas kernels, per_device(): pl.pallas_call(functools.partial(join_kernel, (tm_n, sym_n, cap)), out_sh...  54 us
    mul x1, other arithmetic, per_device(): return trade_size[:, None] * joined  2.53 us

profile of v2, /device:TPU:0, one launch (start us, length us, event | category | flops | bytes accessed | tf_op | source)
XLA Modules:
  0.0 56.5 jit_solution(1644032008287657772)
XLA Ops:
  0.0 0.0 copy-start
  0.0 54.0 %shard_map.73 = f32[2048,128]{1,0:T(8,128)} custom-call(s32[1,2048]{1,0:T(1,128)} %bitcast.5, s32[1,2048]{1,0:T(1,128)} %bitcast.6, s32[1,2048]{1,0:T(1,128)} %bitcast.7, f32[1,2048]{1,0:T(1,128)} %bitcast.8, f32[1,128]{1,0:T(1,128)} %bitcast.9, f32[16,512,128]{2,1,0:T(8,128)} %quotes_ref.1), custom_call_target="tpu_custom_call" | custom-call | tf_op jit(solution)/shard_map/pallas_call | solution.py:227
  54.0 0.0 copy-done
  54.0 2.5 %broadcast_multiply_fusion = f32[2048,128]{1,0:T(8,128)} fusion(f32[2048,128]{1,0:T(8,128)} %shard_map.73, f32[2048]{0:T(1024)S(1)} %copy-done), kind=kLoop, calls=%fused_computation | loop fusion | flops 262144 | bytes 2105344 | tf_op jit(solution)/shard_map/mul | solution.py:257
Async XLA Ops:
  0.0 54.0 %copy-start = (f32[2048]{0:T(1024)S(1)}, f32[2048]{0:T(1024)}, u32[]{:S(2)}) copy-start(f32[2048]{0:T(1024)} %param.8) | copy-start | bytes 24580

commit v3 on v2

--- a/solution.py
+++ b/solution.py
@@ -38,10 +38,17 @@
     flip = flips(me, devices)
     group = min(8, devices)
 
+    top = len(flip) - 1
+    half = lax.div(2 * me, devices)
+    quarter = lax.rem(lax.div(4 * me, devices), 2)
+
     def peer(k):
         p = me
         for i, step in enumerate(flip):
-            if k >> i & 1:
+            if i == top - 1 and k >> top & 1:
+                want = 1 - half if k >> i & 1 else half
+                p = p + (want - quarter) * (1 << i)
+            elif k >> i & 1:
                 p = p + step
         return p
 

time: 56.7 us -> 53.9 us (0.951)
  the two profiles are of different devices: /device:TPU:0 before, /device:TPU:9 now
where the time goes in v3:
time: 53.9 us; the launch traced here: 53.7 us
  Pallas kernels  51.1 us (95%)
  other arithmetic  2.53 us (5%)
    pallas_call x1, Pallas kernels, per_device(): pl.pallas_call(functools.partial(join_kernel, (tm_n, sym_n, cap)), out_sh...  51.1 us
    mul x1, other arithmetic, per_device(): return trade_size[:, None] * joined  2.53 us

profile of v3, /device:TPU:9, one launch (start us, length us, event | category | flops | bytes accessed | tf_op | source)
XLA Modules:
  0.0 53.7 jit_solution(6467886966804933016)
XLA Ops:
  0.0 0.0 copy-start
  0.0 51.1 %shard_map.73 = f32[2048,128]{1,0:T(8,128)} custom-call(s32[1,2048]{1,0:T(1,128)} %bitcast.5, s32[1,2048]{1,0:T(1,128)} %bitcast.6, s32[1,2048]{1,0:T(1,128)} %bitcast.7, f32[1,2048]{1,0:T(1,128)} %bitcast.8, f32[1,128]{1,0:T(1,128)} %bitcast.9, f32[16,512,128]{2,1,0:T(8,128)} %quotes_ref.1), custom_call_target="tpu_custom_call" | custom-call | tf_op jit(solution)/shard_map/pallas_call | solution.py:234
  51.1 0.0 copy-done
  51.2 2.5 %broadcast_multiply_fusion = f32[2048,128]{1,0:T(8,128)} fusion(f32[2048,128]{1,0:T(8,128)} %shard_map.73, f32[2048]{0:T(1024)S(1)} %copy-done), kind=kLoop, calls=%fused_computation | loop fusion | flops 262144 | bytes 2105344 | tf_op jit(solution)/shard_map/mul | solution.py:264
Async XLA Ops:
  0.0 51.2 %copy-start = (f32[2048]{0:T(1024)S(1)}, f32[2048]{0:T(1024)}, u32[]{:S(2)}) copy-start(f32[2048]{0:T(1024)} %param.8) | copy-start | bytes 24580
